TPU v7x, 32 devices: a whole 2x2x4 slice. The times are simulated.
32 devices in a mesh: head: 4 (over y, core), seq: 8 (over z, x).
Axes of the slice: x: 2, y: 2, z: 4, core: 2. Of those that a mesh axis runs over, the one named last changes fastest.
Arguments:
- cached_keys: bfloat16 [8, 32768, 8, 128], P(None, 'seq', 'head'), may hold values from -6 to 6
- queries: bfloat16 [8, 64, 128], P('seq', 'head'), may hold values from -6 to 6
- seq_lengths: int32 [8], replicated, may hold values from 1 to 32768
Outputs:
- page_min: bfloat16 [8, 2048, 8, 128], P('seq', 'head')
- page_max: bfloat16 [8, 2048, 8, 128], P('seq', 'head')
- page_mean: float32 [8, 2048, 8, 128], P('seq', 'head')
- page_score: float32 [8, 64, 2048], P('seq', None, 'head')
All inputs are finite; a program needn't handle non-finite values.
Results may differ from a plain program's by a relative error of at most 0.001.
Values may be sent and summed in bfloat16 or wider, within the bound.
A program may use at most 192 MiB of HBM per device.

v0:
```python
import jax
import jax.numpy as jnp
from jax import lax
from jax.sharding import PartitionSpec as P

PAGE = 16


def page_bounds(block, start, limit):
    seq_count = block.shape[0]
    tokens = block.shape[1]
    position = start + jnp.arange(tokens, dtype=jnp.int32)
    live_token = (position[None, :] < limit[:, None])[:, :, None, None]
    shaped = (seq_count, tokens // PAGE, PAGE, block.shape[2], block.shape[3])
    top_value = jnp.array(jnp.inf, block.dtype)
    lower = jnp.min(jnp.where(live_token, block, top_value).reshape(shaped), axis=2)
    upper = jnp.max(jnp.where(live_token, block, -top_value).reshape(shaped), axis=2)
    key_sums = jnp.sum(
        jnp.where(live_token, block, jnp.zeros((), block.dtype)).reshape(shaped),
        axis=2,
        dtype=jnp.float32,
    )
    page_start = start + PAGE * jnp.arange(tokens // PAGE, dtype=jnp.int32)
    page_live = (page_start[None, :] < limit[:, None])[:, :, None, None]
    zero_value = jnp.zeros((), block.dtype)
    lower = jnp.where(page_live, lower, zero_value)
    upper = jnp.where(page_live, upper, zero_value)
    return (lower, upper, key_sums)


def page_average(key_sums, start, limit):
    page_start = start + PAGE * jnp.arange(key_sums.shape[1], dtype=jnp.int32)
    counts = jnp.clip(limit[:, None] - page_start[None, :], 0, PAGE).astype(jnp.float32)
    return key_sums / jnp.maximum(counts, 1.0)[:, :, None, None]


def bound_scores(query, lower, upper):
    seq_count, heads, width = query.shape
    kv_heads = lower.shape[2]
    grouped = query.astype(jnp.float32).reshape(seq_count, kv_heads, heads // kv_heads, width)
    positive = jnp.maximum(grouped, 0.0)
    negative = jnp.minimum(grouped, 0.0)
    score = jnp.einsum(
        "shgc,sphc->shgp", positive, upper.astype(jnp.float32), precision=lax.Precision.HIGHEST
    )
    score = score + jnp.einsum(
        "shgc,sphc->shgp", negative, lower.astype(jnp.float32), precision=lax.Precision.HIGHEST
    )
    return score.reshape(seq_count, heads, lower.shape[1]) * width ** (-0.5)


def local(cached_keys, queries, seq_lengths):
    seq_index = lax.axis_index("seq")
    head_index = lax.axis_index("head")
    local_seqs = cached_keys.shape[0] // lax.axis_size("seq")
    block_tokens = cached_keys.shape[1]
    quarter = block_tokens * lax.axis_size("seq") // lax.axis_size("head")
    first_token = head_index * quarter
    my_lengths = lax.dynamic_slice_in_dim(seq_lengths, seq_index * local_seqs, local_seqs)
    block_start = seq_index * block_tokens
    lower, upper, key_sums = page_bounds(cached_keys, block_start, seq_lengths)
    lower, upper = (
        lax.all_to_all(
            lax.all_to_all(lower, "seq", split_axis=0, concat_axis=1, tiled=True),
            "head",
            split_axis=1,
            concat_axis=2,
            tiled=True,
        ),
        lax.all_to_all(
            lax.all_to_all(upper, "seq", split_axis=0, concat_axis=1, tiled=True),
            "head",
            split_axis=1,
            concat_axis=2,
            tiled=True,
        ),
    )
    key_sums = lax.all_to_all(
        lax.all_to_all(key_sums, "seq", split_axis=0, concat_axis=1, tiled=True),
        "head",
        split_axis=1,
        concat_axis=2,
        tiled=True,
    )
    average = page_average(key_sums, first_token, my_lengths)
    whole_query = lax.all_gather(queries, "head", axis=1, tiled=True)
    score = bound_scores(whole_query, lower, upper)
    return (lower, upper, average, score)


def solution(mesh):
    return jax.shard_map(
        local,
        mesh=mesh,
        in_specs=(P(None, "seq", "head", None), P("seq", "head", None), P()),
        out_specs=(
            P("seq", "head", None, None),
            P("seq", "head", None, None),
            P("seq", "head", None, None),
            P("seq", None, "head"),
        ),
        check_vma=False,
    )
```

profile of v0, /device:TPU:19, one launch (start us, length us, event | category | flops | bytes accessed | tf_op | source)
XLA Modules:
  0.0 335.3 jit_solution(6513787656820091344)
XLA Ops:
  0.7 0.7 broadcast_compare_fusion
  1.4 0.7 broadcast_compare_fusion.1
  2.1 98.4 %broadcast_select_fusion = (bf16[8,4096,2,128]{3,2,1,0:T(2,128)(2,1)}, bf16[8,4096,2,128]{3,2,1,0:T(2,128)(2,1)}, bf16[8,4096,2,128]{3,2,1,0:T(2,128)(2,1)}) fusion(bf16[8,4096,2,128]{3,2,1,0:T(2,128)(2,1)} %param.3, pred[8,4096]{1,0:T(8,128)(4,1)S(1)} %broadcast_compare_fusion), kind=kLoop, calls=%fused_computation.1 | loop fusion | flops 25165824 | bytes 67141632 | tf_op jit(solution)/shard_map/jit(_where)/select_n | solution.py:19
  100.6 18.6 %reduce_max.9 = bf16[8,256,2,128]{3,2,1,0:T(2,128)(2,1)S(1)} reduce(bf16[8,256,16,2,128]{4,3,2,1,0:T(2,128)(2,1)} %bitcast.33, bf16[]{:T(256)} %constant.4.clone.1), dimensions={2}, to_apply=%region_1.2 | reduce | flops 7864320 | bytes 17825794 | tf_op jit(solution)/shard_map/reduce_max | solution.py:17
  119.2 18.6 %reduce_min.9 = bf16[8,256,2,128]{3,2,1,0:T(2,128)(2,1)S(1)} reduce(bf16[8,256,16,2,128]{4,3,2,1,0:T(2,128)(2,1)} %bitcast.32, bf16[]{:T(256)} %constant.16.clone.1), dimensions={2}, to_apply=%region_0.1 | reduce | flops 7864320 | bytes 17825794 | tf_op jit(solution)/shard_map/reduce_min | solution.py:16
  137.8 2.9 broadcast_select_fusion.3
  140.7 1.2 copy.38
  141.9 5.5 %all-to-all-start.2 = ((bf16[8,256,2,128]{3,1,2,0:T(8,128)(2,1)}), bf16[8,256,2,128]{3,1,2,0:T(8,128)(2,1)S(1)}, u32[]{:S(2)}, u32[]{:S(2)}) async-start(bf16[8,256,2,128]{3,1,2,0:T(8,128)(2,1)} %copy.38), calls=%async_computation.2 | async-start | bytes 2097152 | tf_op jit(solution)/shard_map/all_to_all | solution.py:71
  147.4 1.2 copy.33
  148.6 21.1 %all-to-all-done.2 = bf16[8,256,2,128]{3,1,2,0:T(8,128)(2,1)S(1)} async-done(((bf16[8,256,2,128]{3,1,2,0:T(8,128)(2,1)}), bf16[8,256,2,128]{3,1,2,0:T(8,128)(2,1)S(1)}, u32[]{:S(2)}, u32[]{:S(2)}) %all-to-all-start.2) | async-done | bytes 1048608 | tf_op jit(solution)/shard_map/all_to_all | solution.py:71
  169.7 7.3 %all-to-all-start = ((bf16[8,256,2,128]{3,1,2,0:T(8,128)(2,1)}), bf16[8,256,2,128]{3,1,2,0:T(8,128)(2,1)S(1)}, u32[]{:S(2)}, u32[]{:S(2)}) async-start(bf16[8,256,2,128]{3,1,2,0:T(8,128)(2,1)} %copy.33), calls=%async_computation | async-start | bytes 2097152 | tf_op jit(solution)/shard_map/all_to_all | solution.py:64
  177.0 0.1 copy.39
  177.1 9.5 %copy.40 = bf16[1,2048,2,128]{3,2,0,1:T(2,128)(2,1)} copy(bf16[1,2048,2,128]{3,1,2,0:T(8,128)(2,1)S(1)} %bitcast.42) | data formatting | bytes 2097152 | tf_op jit(solution)/shard_map/all_to_all | solution.py:71
  186.5 12.7 %all-to-all-done = bf16[8,256,2,128]{3,1,2,0:T(8,128)(2,1)S(1)} async-done(((bf16[8,256,2,128]{3,1,2,0:T(8,128)(2,1)}), bf16[8,256,2,128]{3,1,2,0:T(8,128)(2,1)S(1)}, u32[]{:S(2)}, u32[]{:S(2)}) %all-to-all-start) | async-done | bytes 1048608 | tf_op jit(solution)/shard_map/all_to_all | solution.py:64
  199.3 4.9 %all-to-all-start.3 = ((bf16[1,2048,2,128]{3,2,0,1:T(2,128)(2,1)}), bf16[1,2048,2,128]{3,2,0,1:T(2,128)(2,1)S(1)}, u32[]{:S(2)}, u32[]{:S(2)}) async-start(bf16[1,2048,2,128]{3,2,0,1:T(2,128)(2,1)} %copy.40), calls=%async_computation.3 | async-start | bytes 2097152 | tf_op jit(solution)/shard_map/all_to_all | solution.py:70
  204.1 0.0 copy-done
  204.1 16.8 %convert_reduce_fusion = f32[8,256,2,128]{3,2,1,0:T(2,128)S(1)} fusion(bf16[8,256,16,2,128]{4,3,2,1,0:T(2,128)(2,1)} %bitcast.34), kind=kLoop, calls=%fused_computation | loop fusion | flops 16252928 | bytes 18874368 | tf_op jit(solution)/shard_map/reduce_sum | solution.py:18
  221.0 0.0 copy-start.2
  221.0 0.0 copy-start.1
  221.0 1.5 copy.43
  222.5 0.0 all-to-all-done.3
  222.5 6.6 %all-to-all-start.4 = ((f32[8,256,2,128]{3,1,2,0:T(8,128)}), f32[8,256,2,128]{3,1,2,0:T(8,128)S(1)}, u32[]{:S(2)}, u32[]{:S(2)}) async-start(f32[8,256,2,128]{3,1,2,0:T(8,128)} %copy.43), calls=%async_computation.4 | async-start | bytes 4194304 | tf_op jit(solution)/shard_map/all_to_all | solution.py:79
  229.1 1.3 copy.34
  230.4 9.5 %copy.35 = bf16[1,2048,2,128]{3,2,0,1:T(2,128)(2,1)} copy(bf16[1,2048,2,128]{3,1,2,0:T(8,128)(2,1)S(1)} %bitcast.43) | data formatting | bytes 2097152 | tf_op jit(solution)/shard_map/all_to_all | solution.py:64
  239.9 34.3 %all-to-all-done.4 = f32[8,256,2,128]{3,1,2,0:T(8,128)S(1)} async-done(((f32[8,256,2,128]{3,1,2,0:T(8,128)}), f32[8,256,2,128]{3,1,2,0:T(8,128)S(1)}, u32[]{:S(2)}, u32[]{:S(2)}) %all-to-all-start.4) | async-done | bytes 2097184 | tf_op jit(solution)/shard_map/all_to_all | solution.py:79
  274.1 5.4 %all-to-all-start.1 = ((bf16[1,2048,2,128]{3,2,0,1:T(2,128)(2,1)}), bf16[1,2048,2,128]{3,2,0,1:T(2,128)(2,1)}, u32[]{:S(2)}, u32[]{:S(2)}) async-start(bf16[1,2048,2,128]{3,2,0,1:T(2,128)(2,1)} %copy.35), calls=%async_computation.1 | async-start | bytes 2097152 | tf_op jit(solution)/shard_map/all_to_all | solution.py:63
  279.5 0.2 copy.44
  279.7 8.6 %copy.45 = f32[1,2048,2,128]{3,2,0,1:T(2,128)} copy(f32[1,2048,2,128]{3,1,2,0:T(8,128)S(1)} %bitcast.40) | data formatting | bytes 4194304 | tf_op jit(solution)/shard_map/all_to_all | solution.py:79
  288.2 4.9 %all-to-all-done.1 = bf16[1,2048,2,128]{3,2,0,1:T(2,128)(2,1)} async-done(((bf16[1,2048,2,128]{3,2,0,1:T(2,128)(2,1)}), bf16[1,2048,2,128]{3,2,0,1:T(2,128)(2,1)}, u32[]{:S(2)}, u32[]{:S(2)}) %all-to-all-start.1) | async-done | bytes 1048608 | tf_op jit(solution)/shard_map/all_to_all | solution.py:63
  293.1 4.5 %all-to-all-start.5 = ((f32[1,2048,2,128]{3,2,0,1:T(2,128)}), f32[1,2048,2,128]{3,2,0,1:T(2,128)S(1)}, u32[]{:S(2)}, u32[]{:S(2)}) async-start(f32[1,2048,2,128]{3,2,0,1:T(2,128)} %copy.45), calls=%async_computation.5 | async-start | bytes 4194304 | tf_op jit(solution)/shard_map/all_to_all | solution.py:78
  297.6 0.0 copy-done.2
  297.6 0.6 dynamic_slice.3
  298.2 0.0 copy-done.1
  298.2 25.9 %all_gather.3 = bf16[1,64,128]{2,1,0:T(8,128)(2,1)S(1)} all-gather(bf16[1,16,128]{2,1,0:T(8,128)(2,1)S(1)} %copy-done.1), channel_id=1, replica_groups=mesh['head'=4,'seq'=8] {'head'}, dimensions={1}, use_global_device_ids=true | all-gather | bytes 20480 | tf_op jit(solution)/shard_map/all_gather | solution.py:86
  324.2 0.7 convert_maximum_fusion.1
  324.8 0.1 copy.41
  325.0 0.1 copy.42
  325.0 1.4 copy.36
  326.4 0.1 copy.37
  326.5 1.6 copy.50
  328.1 1.6 copy.51
  329.8 0.9 fusion.3
  330.7 1.6 fusion.1
  332.3 0.0 all-to-all-done.5
  332.3 0.1 copy.46
  332.4 0.1 copy.47
  332.6 0.2 broadcast_divide_fusion
  332.8 2.5 copy.52
  (3 shorter events, 0.0 us)
Async XLA Ops:
  141.9 27.8 %all-to-all-start.2 = ((bf16[8,256,2,128]{3,1,2,0:T(8,128)(2,1)}), bf16[8,256,2,128]{3,1,2,0:T(8,128)(2,1)S(1)}, u32[]{:S(2)}, u32[]{:S(2)}) async-start(bf16[8,256,2,128]{3,1,2,0:T(8,128)(2,1)} %copy.38), calls=%async_computation.2 | async-start | bytes 2097152 | tf_op jit(solution)/shard_map/all_to_all | solution.py:71
  169.7 29.5 %all-to-all-start = ((bf16[8,256,2,128]{3,1,2,0:T(8,128)(2,1)}), bf16[8,256,2,128]{3,1,2,0:T(8,128)(2,1)S(1)}, u32[]{:S(2)}, u32[]{:S(2)}) async-start(bf16[8,256,2,128]{3,1,2,0:T(8,128)(2,1)} %copy.33), calls=%async_computation | async-start | bytes 2097152 | tf_op jit(solution)/shard_map/all_to_all | solution.py:64
  199.3 4.9 %copy-start = (bf16[8,256,2,128]{3,1,2,0:T(8,128)(2,1)}, bf16[8,256,2,128]{3,1,2,0:T(8,128)(2,1)S(1)}, u32[]{:S(2)}) copy-start(bf16[8,256,2,128]{3,1,2,0:T(8,128)(2,1)S(1)} %all-to-all-done) | copy-start | bytes 3145732
  199.3 23.3 %all-to-all-start.3 = ((bf16[1,2048,2,128]{3,2,0,1:T(2,128)(2,1)}), bf16[1,2048,2,128]{3,2,0,1:T(2,128)(2,1)S(1)}, u32[]{:S(2)}, u32[]{:S(2)}) async-start(bf16[1,2048,2,128]{3,2,0,1:T(2,128)(2,1)} %copy.40), calls=%async_computation.3 | async-start | bytes 2097152 | tf_op jit(solution)/shard_map/all_to_all | solution.py:70
  221.0 76.7 %copy-start.2 = (s32[8]{0:T(128)S(1)}, s32[8]{0:T(128)}, u32[]{:S(2)}) copy-start(s32[8]{0:T(128)} %param.5) | copy-start | bytes 100
  221.0 77.2 %copy-start.1 = (bf16[1,16,128]{2,1,0:T(8,128)(2,1)S(1)}, bf16[1,16,128]{2,1,0:T(8,128)(2,1)}, u32[]{:S(2)}) copy-start(bf16[1,16,128]{2,1,0:T(8,128)(2,1)} %param.4) | copy-start | bytes 12292
  222.5 51.6 %all-to-all-start.4 = ((f32[8,256,2,128]{3,1,2,0:T(8,128)}), f32[8,256,2,128]{3,1,2,0:T(8,128)S(1)}, u32[]{:S(2)}, u32[]{:S(2)}) async-start(f32[8,256,2,128]{3,1,2,0:T(8,128)} %copy.43), calls=%async_computation.4 | async-start | bytes 4194304 | tf_op jit(solution)/shard_map/all_to_all | solution.py:79
  274.1 19.0 %all-to-all-start.1 = ((bf16[1,2048,2,128]{3,2,0,1:T(2,128)(2,1)}), bf16[1,2048,2,128]{3,2,0,1:T(2,128)(2,1)}, u32[]{:S(2)}, u32[]{:S(2)}) async-start(bf16[1,2048,2,128]{3,2,0,1:T(2,128)(2,1)} %copy.35), calls=%async_computation.1 | async-start | bytes 2097152 | tf_op jit(solution)/shard_map/all_to_all | solution.py:63
  293.1 39.2 %all-to-all-start.5 = ((f32[1,2048,2,128]{3,2,0,1:T(2,128)}), f32[1,2048,2,128]{3,2,0,1:T(2,128)S(1)}, u32[]{:S(2)}, u32[]{:S(2)}) async-start(f32[1,2048,2,128]{3,2,0,1:T(2,128)} %copy.45), calls=%async_computation.5 | async-start | bytes 4194304 | tf_op jit(solution)/shard_map/all_to_all | solution.py:78
where the time goes:
time: 340 us; the launch traced here: 335 us
  other arithmetic  158 us (46%)
  waiting for transfers between devices  73 us (21%)
  local copies, waits for them, and re-layouts  41.3 us (12%)
  starting transfers between devices  34.2 us (10%)
  blocking collectives  25.9 us (8%)
    select_n x1, other arithmetic, page_bounds(): jnp.where(live_token, block, jnp.zeros((), block.dtype)).reshape(shaped)  98.4 us
    all_to_all x1, waiting for transfers between devices, local(): lax.all_to_all(key_sums, 'seq', split_axis=0, concat_axis=1, tiled=True)  34.3 us
    all_gather x1, blocking collectives, local(): whole_query = lax.all_gather(queries, 'head', axis=1, tiled=True)  25.9 us
    all_to_all x1, waiting for transfers between devices, local(): lax.all_to_all(upper, 'seq', split_axis=0, concat_axis=1, tiled=True)  21.1 us
    reduce_min x1, other arithmetic, page_bounds(): jnp.min(jnp.where(live_token, block, top_value).reshape(shaped), axis=2)  18.6 us
    reduce_max x1, other arithmetic, page_bounds(): jnp.max(jnp.where(live_token, block, -top_value).reshape(shaped), axis=2)  18.6 us
    reduce_sum x1, other arithmetic, page_bounds(): jnp.sum(jnp.where(live_token, block, jnp.zeros((), block.dtype)).reshape(...  16.8 us
    all_to_all x1, waiting for transfers between devices, local(): lax.all_to_all(lower, 'seq', split_axis=0, concat_axis=1, tiled=True)  12.7 us
  transfers between devices with their start and end apart: 6, of which 4 were waited for; matrix products, arithmetic and copies ran while one was open for 17% of the time, Pallas kernels for 0%

commit v1 on v0

v1 whole, which is shorter than its diff:
```python
import functools

import jax
import jax.numpy as jnp
from jax import lax
from jax.experimental import pallas as pl
from jax.experimental.pallas import tpu as pltpu
from jax.sharding import PartitionSpec as P

PAGE = 16
SLOTS = 3
MESH = pl.DeviceIdType.MESH
SPAN = 28.0
TOP = 32767.0


def page_kernel(
    seqs, heads, lengths, keys, query, low_out, high_out, sum_out, query_out,
    buf, low, high, code, key_sem, send_sem, recv_sem, own_sem, query_send, query_recv, query_own,
):
    head = lax.axis_index("head")
    seq = lax.axis_index("seq")
    ratio = seqs // heads
    pages = keys.shape[1]
    width = keys.shape[3]
    lanes = keys.shape[4]
    rows = pages * width
    chunk = min(64, rows)
    owner = seq // ratio
    part = lax.rem(seq, ratio)
    mine = owner == head

    def dest_of(step):
        return lax.rem(seq + lax.rem(step + seqs // 2, seqs), seqs)

    def fetch(step):
        slot = lax.rem(step, SLOTS)
        dest = dest_of(step)
        for t in range(PAGE):
            pltpu.make_async_copy(keys.at[dest, :, t], buf.at[slot, t], key_sem.at[slot, t]).start()

    for step in range(min(SLOTS - 1, seqs)):
        fetch(jnp.int32(step))

    barrier = pltpu.get_barrier_semaphore()

    def greet(i, carry):
        source_head = i // ratio
        source_seq = head * ratio + lax.rem(i, ratio)

        @pl.when(jnp.logical_or(source_head != head, source_seq != seq))
        def _():
            pl.semaphore_signal(barrier, inc=1, device_id=(source_head, source_seq), device_id_type=MESH)

        return carry

    lax.fori_loop(0, seqs, greet, 0)
    for i in range(1, heads):
        pl.semaphore_signal(barrier, inc=1, device_id=(lax.rem(head + i, heads), seq), device_id_type=MESH)
    expected = seqs - jnp.where(mine, 1, 0) + heads - 1
    pl.semaphore_wait(barrier, expected)

    def query_copy(i, target):
        return pltpu.make_async_remote_copy(
            src_ref=query, dst_ref=query_out.at[head], send_sem=query_send.at[i], recv_sem=query_recv.at[i],
            device_id=(target, seq), device_id_type=MESH,
        )

    for i in range(heads - 1):
        query_copy(i, lax.rem(head + i + 1, heads)).start()
    own_query = pltpu.make_async_copy(query, query_out.at[head], query_own)
    own_query.start()

    trio = ((low, low_out), (high, high_out), (code, sum_out))
    index = head * ratio + part

    def remote(step, k):
        source, target = trio[k]
        return pltpu.make_async_remote_copy(
            src_ref=source.at[step],
            dst_ref=target.at[pl.ds(part * pages, pages), head],
            send_sem=send_sem.at[step, k],
            recv_sem=recv_sem.at[index, k],
            device_id=(owner, dest_of(step)),
            device_id_type=MESH,
        )

    def local(step, k):
        source, target = trio[k]
        return pltpu.make_async_copy(source.at[step], target.at[pl.ds(part * pages, pages), head], own_sem.at[k])

    def work(step, carry):
        @pl.when(step + SLOTS - 1 < seqs)
        def _():
            fetch(step + SLOTS - 1)

        slot = lax.rem(step, SLOTS)
        dest = dest_of(step)
        for t in range(PAGE):
            pltpu.make_async_copy(keys.at[dest, :, t], buf.at[slot, t], key_sem.at[slot, t]).wait()
        block = buf.at[slot]
        flat = block.reshape(PAGE, rows, lanes)
        limit = lengths[dest] - seq * (pages * PAGE)
        row = lax.broadcasted_iota(jnp.int32, (chunk, lanes), 0)
        token = (row // width) * PAGE
        low_flat = low.at[step].reshape(rows, lanes)
        high_flat = high.at[step].reshape(rows, lanes)
        code_flat = code.at[step].reshape(rows, lanes)

        def piece(c, carry):
            at = pl.ds(pl.multiple_of(c * chunk, chunk), chunk)
            left = limit - c * (chunk // width * PAGE)
            small = jnp.full((chunk, lanes), jnp.inf, jnp.float32)
            large = jnp.full((chunk, lanes), -jnp.inf, jnp.float32)
            total = jnp.zeros((chunk, lanes), jnp.float32)
            for t in range(PAGE):
                x = flat[t, at, :].astype(jnp.float32)
                keep = token < left - t
                small = jnp.where(keep, jnp.minimum(small, x), small)
                large = jnp.where(keep, jnp.maximum(large, x), large)
                total = jnp.where(keep, total + x, total)
            live = token < left
            small = jnp.where(live, small, 0.0)
            large = jnp.where(live, large, 0.0)
            bound = jnp.maximum(jnp.abs(small), jnp.abs(large))
            share = jnp.abs(total) / (PAGE * jnp.where(bound > 0.0, bound, 1.0))
            level = jnp.log2(jnp.maximum(share, 1e-30)) * (TOP / SPAN) + TOP
            level = jnp.clip(level + 0.5, 0.0, TOP)
            level = jnp.where(total < 0.0, -level, level)
            low_flat[at, :] = small.astype(low.dtype)
            high_flat[at, :] = large.astype(high.dtype)
            code_flat[at, :] = level.astype(jnp.int32).astype(jnp.int16)
            return carry

        lax.fori_loop(0, rows // chunk, piece, 0)
        itself = jnp.logical_and(mine, dest == seq)

        @pl.when(itself)
        def _():
            for k in range(3):
                local(step, k).start()

        @pl.when(jnp.logical_not(itself))
        def _():
            for k in range(3):
                remote(step, k).start()

        return carry

    lax.fori_loop(0, seqs, work, 0)

    for i in range(heads - 1):
        query_copy(i, lax.rem(head + i + 1, heads)).wait()
    own_query.wait()

    def finish(step, carry):
        itself = jnp.logical_and(mine, dest_of(step) == seq)

        @pl.when(itself)
        def _():
            for k in range(3):
                local(step, k).wait()

        @pl.when(jnp.logical_not(itself))
        def _():
            for k in range(3):
                remote(step, k).wait_send()

        return carry

    lax.fori_loop(0, seqs, finish, 0)

    def arrive(i, carry):
        source_head = i // ratio
        source_part = lax.rem(i, ratio)
        itself = jnp.logical_and(source_head == head, head * ratio + source_part == seq)

        @pl.when(jnp.logical_not(itself))
        def _():
            for k in range(3):
                source, target = trio[k]
                pltpu.make_async_remote_copy(
                    src_ref=source.at[0],
                    dst_ref=target.at[pl.ds(source_part * pages, pages), source_head],
                    send_sem=send_sem.at[0, k],
                    recv_sem=recv_sem.at[i, k],
                    device_id=(source_head, head * ratio + source_part),
                    device_id_type=MESH,
                ).wait_recv()

        return carry

    lax.fori_loop(0, seqs, arrive, 0)


def score_kernel(lengths, low, high, code, query, low_out, high_out, mean_out, score_out):
    block, kv_heads, lanes = low.shape
    count_q = query.shape[0]
    total_pages = block * pl.num_programs(0)
    start = lax.axis_index("head") * total_pages + pl.program_id(0) * block
    limit = lengths[lax.axis_index("seq")]
    small = low[...]
    large = high[...]
    low_out[0] = small
    high_out[0] = large
    bound = jnp.maximum(jnp.abs(small.astype(jnp.float32)), jnp.abs(large.astype(jnp.float32)))
    level = code[...].astype(jnp.int32).astype(jnp.float32)
    share = jnp.exp2((jnp.abs(level) - TOP) * (SPAN / TOP))
    total = jnp.where(level == 0.0, 0.0, share * (PAGE * bound))
    total = jnp.where(level < 0.0, -total, total)
    page = start + lax.broadcasted_iota(jnp.int32, (block, kv_heads, lanes), 0)
    count = jnp.clip(limit - page * PAGE, 1, PAGE).astype(jnp.float32)
    mean_out[0] = total / count
    q = query[...].astype(jnp.float32)
    positive = jnp.maximum(q, 0.0).astype(jnp.bfloat16)
    negative = jnp.minimum(q, 0.0).astype(jnp.bfloat16)
    dims = (((1,), (1,)), ((), ()))
    both = lax.dot_general(
        large.reshape(block * kv_heads, lanes), positive, dims, preferred_element_type=jnp.float32
    ) + lax.dot_general(
        small.reshape(block * kv_heads, lanes), negative, dims, preferred_element_type=jnp.float32
    )
    both = both.reshape(block, kv_heads, count_q)
    kv = lax.broadcasted_iota(jnp.int32, both.shape, 1)
    of = lax.broadcasted_iota(jnp.int32, both.shape, 2) // (count_q // kv_heads)
    score = jnp.sum(jnp.where(kv == of, both, 0.0), axis=1) * lanes ** (-0.5)
    score_out[0] = score.T


def local_step(heads, seqs, cached_keys, queries, seq_lengths):
    seq_count, tokens, width, lanes = cached_keys.shape
    pages = tokens // PAGE
    owned = pages * seqs // heads
    local_q = queries.shape[1]
    keys = cached_keys.reshape(seq_count, pages, PAGE, width, lanes)
    any_space = pl.BlockSpec(memory_space=pl.ANY)
    shape = (owned, heads, width, lanes)
    low, high, code, query = pl.pallas_call(
        functools.partial(page_kernel, seqs, heads),
        out_shape=(
            jax.ShapeDtypeStruct(shape, jnp.bfloat16),
            jax.ShapeDtypeStruct(shape, jnp.bfloat16),
            jax.ShapeDtypeStruct(shape, jnp.int16),
            jax.ShapeDtypeStruct((heads, local_q, lanes), jnp.bfloat16),
        ),
        in_specs=[pl.BlockSpec(memory_space=pltpu.SMEM), any_space, any_space],
        out_specs=(any_space,) * 4,
        scratch_shapes=[
            pltpu.VMEM((SLOTS, PAGE, pages, width, lanes), jnp.bfloat16),
            pltpu.VMEM((seqs, pages, width, lanes), jnp.bfloat16),
            pltpu.VMEM((seqs, pages, width, lanes), jnp.bfloat16),
            pltpu.VMEM((seqs, pages, width, lanes), jnp.int16),
            pltpu.SemaphoreType.DMA((SLOTS, PAGE)),
            pltpu.SemaphoreType.DMA((seqs, 3)),
            pltpu.SemaphoreType.DMA((seqs, 3)),
            pltpu.SemaphoreType.DMA((3,)),
            pltpu.SemaphoreType.DMA((heads - 1,)),
            pltpu.SemaphoreType.DMA((heads - 1,)),
            pltpu.SemaphoreType.DMA,
        ],
        compiler_params=pltpu.CompilerParams(collective_id=0, has_side_effects=True),
        name="page_exchange",
    )(seq_lengths, keys, queries.reshape(local_q, lanes))
    kv_heads = heads * width
    count_q = heads * local_q
    block = min(128, owned)
    page_spec = pl.BlockSpec((block, kv_heads, lanes), lambda i: (i, 0, 0))
    out_spec = pl.BlockSpec((1, block, kv_heads, lanes), lambda i: (0, i, 0, 0))
    whole = (1, owned, kv_heads, lanes)
    return pl.pallas_call(
        score_kernel,
        grid=(owned // block,),
        out_shape=(
            jax.ShapeDtypeStruct(whole, jnp.bfloat16),
            jax.ShapeDtypeStruct(whole, jnp.bfloat16),
            jax.ShapeDtypeStruct(whole, jnp.float32),
            jax.ShapeDtypeStruct((1, count_q, owned), jnp.float32),
        ),
        in_specs=[
            pl.BlockSpec(memory_space=pltpu.SMEM),
            page_spec,
            page_spec,
            page_spec,
            pl.BlockSpec((count_q, lanes), lambda i: (0, 0)),
        ],
        out_specs=(out_spec, out_spec, out_spec, pl.BlockSpec((1, count_q, block), lambda i: (0, 0, i))),
        name="page_score",
    )(
        seq_lengths,
        low.reshape(owned, kv_heads, lanes),
        high.reshape(owned, kv_heads, lanes),
        code.reshape(owned, kv_heads, lanes),
        query.reshape(count_q, lanes),
    )


def solution(mesh):
    return jax.shard_map(
        functools.partial(local_step, mesh.shape["head"], mesh.shape["seq"]),
        mesh=mesh,
        in_specs=(P(None, "seq", "head", None), P("seq", "head", None), P()),
        out_specs=(
            P("seq", "head", None, None),
            P("seq", "head", None, None),
            P("seq", "head", None, None),
            P("seq", None, "head"),
        ),
        check_vma=False,
    )
```

time: 340 us -> 89.6 us (0.26); the launches traced: 335 us -> 89.4 us
  other arithmetic: 158 us -> 0 us
  Pallas kernels: 0 us -> 88.7 us
  waiting for transfers between devices: 73 us -> 0 us
  local copies, waits for them, and re-layouts: 41.3 us -> 0 us
  starting transfers between devices: 34.2 us -> 0 us
  blocking collectives: 25.9 us -> 0 us
    select_n x2 -> x0, other arithmetic: 101 us -> none  [the longest x1 98.4 us: page_bounds(): jnp.where(live_token, block, jnp.zeros((), block.dtype)).reshape(shaped)]
    pallas_call x0 -> x2, Pallas kernels: none -> 88.7 us  [the longest x1 82.7 us: local_step(): pl.pallas_call(functools.partial(page_kernel, seqs, heads), out_shape=(ja...]
    all_to_all x6 -> x0, waiting for transfers between devices: 73 us -> none  [the longest x1 34.3 us: local(): lax.all_to_all(key_sums, 'seq', split_axis=0, concat_axis=1, tiled=True)]
    all_to_all x6 -> x0, starting transfers between devices: 34.2 us -> none  [the longest x1 7.25 us: local(): lax.all_to_all(lower, 'seq', split_axis=0, concat_axis=1, tiled=True)]
    all_to_all x12 -> x0, local copies, waits for them, and re-layouts: 30.9 us -> none  [the longest x2 10.8 us: local(): lax.all_to_all(lower, 'seq', split_axis=0, concat_axis=1, tiled=True)]
    all_gather x1 -> x0, blocking collectives: 25.9 us -> none  [local(): whole_query = lax.all_gather(queries, 'head', axis=1, tiled=True)]
    reduce_min x1 -> x0, other arithmetic: 18.6 us -> none  [page_bounds(): jnp.min(jnp.where(live_token, block, top_value).reshape(shaped), axis=2)]
    reduce_max x1 -> x0, other arithmetic: 18.6 us -> none  [page_bounds(): jnp.max(jnp.where(live_token, block, -top_value).reshape(shaped), axis=2)]
  transfers between devices with their start and end apart: 6 -> 0, of which waited for: 4 -> 0; matrix products, arithmetic and copies ran while one was open for 17% -> 0% of each run, Pallas kernels for 0% -> 0%
where the time goes in v1:
time: 89.6 us; the launch traced here: 89.4 us
  Pallas kernels  88.7 us (99%)
    pallas_call x1, Pallas kernels, local_step(): pl.pallas_call(functools.partial(page_kernel, seqs, heads), out_shape=(ja...  82.7 us
    pallas_call x1, Pallas kernels, local_step(): pl.pallas_call(score_kernel, grid=(owned // block,), out_shape=(jax.Shape...  6.03 us

profile of v1, /device:TPU:19, one launch (start us, length us, event | category | flops | bytes accessed | tf_op | source)
XLA Modules:
  0.0 89.4 jit_solution(885410748543951286)
XLA Ops:
  0.6 82.7 %page_exchange.1 = (bf16[512,4,2,128]{3,2,1,0:T(2,128)(2,1)}, bf16[512,4,2,128]{3,2,1,0:T(2,128)(2,1)}, s16[512,4,2,128]{3,2,1,0:T(2,128)(2,1)}, bf16[4,16,128]{2,1,0:T(8,128)(2,1)}) custom-call(s32[8]{0:T(128)} %lengths.3, bf16[8,256,16,2,128]{4,3,2,1,0:T(2,128)(2,1)} %bitcast.6, bf16[16,128]{1,0:T(8,128)(2,1)} %bitcast.11), custom_call_target="tpu_custom_call" | custom-call | tf_op jit(solution)/shard_map/page_exchange/pallas_call | solution.py:238
  83.3 6.0 %page_score.1 = (bf16[1,512,8,128]{3,2,1,0:T(8,128)(2,1)}, bf16[1,512,8,128]{3,2,1,0:T(8,128)(2,1)}, f32[1,512,8,128]{3,2,1,0:T(8,128)}, f32[1,64,512]{2,1,0:T(8,128)}) custom-call(s32[8]{0:T(128)} %lengths.3, bf16[512,8,128]{2,1,0:T(8,128)(2,1)} %bitcast.7, bf16[512,8,128]{2,1,0:T(8,128)(2,1)} %bitcast.8, s16[512,8,128]{2,1,0:T(8,128)(2,1)} %bitcast.9, ...), custom_call_target="tpu_custom_call" | custom-call | tf_op jit(solution)/shard_map/page_score/pallas_call | solution.py:270

commit v2 on v1

--- a/solution.py
+++ b/solution.py
@@ -30,8 +30,15 @@
     part = lax.rem(seq, ratio)
     mine = owner == head
 
+    upper = owner >= (heads + 1) // 2
+    from_end = jnp.where(upper, heads - 1 - owner, owner)
+
     def dest_of(step):
-        return lax.rem(seq + lax.rem(step + seqs // 2, seqs), seqs)
+        turn = step // ratio
+        ahead = heads - 1 - from_end
+        plane = jnp.where(turn < ahead, from_end + 1 + turn, jnp.where(turn < heads - 1, heads - 2 - turn, from_end))
+        plane = jnp.where(upper, heads - 1 - plane, plane)
+        return plane * ratio + lax.rem(part + step, ratio)
 
     def fetch(step):
         slot = lax.rem(step, SLOTS)

time: 89.6 us -> 93 us (1.038)
  the two profiles are of different devices: /device:TPU:19 before, /device:TPU:4 now
where the time goes in v2:
time: 93 us; the launch traced here: 92.8 us
  Pallas kernels  92.2 us (99%)
    pallas_call x1, Pallas kernels, local_step(): pl.pallas_call(functools.partial(page_kernel, seqs, heads), out_shape=(ja...  86.2 us
    pallas_call x1, Pallas kernels, local_step(): pl.pallas_call(score_kernel, grid=(owned // block,), out_shape=(jax.Shape...  6.03 us

profile of v2, /device:TPU:4, one launch (start us, length us, event | category | flops | bytes accessed | tf_op | source)
XLA Modules:
  0.0 92.8 jit_solution(8984247826513149685)
XLA Ops:
  0.6 86.2 %page_exchange.1 = (bf16[512,4,2,128]{3,2,1,0:T(2,128)(2,1)}, bf16[512,4,2,128]{3,2,1,0:T(2,128)(2,1)}, s16[512,4,2,128]{3,2,1,0:T(2,128)(2,1)}, bf16[4,16,128]{2,1,0:T(8,128)(2,1)}) custom-call(s32[8]{0:T(128)} %lengths.3, bf16[8,256,16,2,128]{4,3,2,1,0:T(2,128)(2,1)} %bitcast.6, bf16[16,128]{1,0:T(8,128)(2,1)} %bitcast.11), custom_call_target="tpu_custom_call" | custom-call | tf_op jit(solution)/shard_map/page_exchange/pallas_call | solution.py:245
  86.8 6.0 %page_score.1 = (bf16[1,512,8,128]{3,2,1,0:T(8,128)(2,1)}, bf16[1,512,8,128]{3,2,1,0:T(8,128)(2,1)}, f32[1,512,8,128]{3,2,1,0:T(8,128)}, f32[1,64,512]{2,1,0:T(8,128)}) custom-call(s32[8]{0:T(128)} %lengths.3, bf16[512,8,128]{2,1,0:T(8,128)(2,1)} %bitcast.7, bf16[512,8,128]{2,1,0:T(8,128)(2,1)} %bitcast.8, s16[512,8,128]{2,1,0:T(8,128)(2,1)} %bitcast.9, ...), custom_call_target="tpu_custom_call" | custom-call | tf_op jit(solution)/shard_map/page_score/pallas_call | solution.py:277
